TPU v7x, 32 devices: a whole 2x2x4 slice. The times are simulated.
32 devices in a mesh: dp: 8 (over z, y), section: 4 (over x, core).
Axes of the slice: x: 2, y: 2, z: 4, core: 2. Of those that a mesh axis runs over, the one named last changes fastest.
Arguments:
- patches: bfloat16 [64, 197, 1024], P('dp'), may hold values from -6 to 6
- ln1_gain: float32 [4, 1024], P('section'), may hold values from 0.5 to 1.5
- w_qkv: bfloat16 [4, 1024, 3072], P('section'), may hold values from -1 to 1
- w_out: bfloat16 [4, 1024, 1024], P('section'), may hold values from -0.1875 to 0.1875
- ln2_gain: float32 [4, 1024], P('section'), may hold values from 0.5 to 1.5
- w_fc1: bfloat16 [4, 1024, 2048], P('section'), may hold values from -0.1875 to 0.1875
- w_fc2: bfloat16 [4, 2048, 1024], P('section'), may hold values from -0.125 to 0.125
- final_norm_gain: float32 [1024], replicated, may hold values from 0.5 to 1.5
- w_head: bfloat16 [1024, 256], replicated, may hold values from -0.1875 to 0.1875
- online_embeddings: bfloat16 [64, 256], P('dp'), may hold values from -60 to 60
- queue: bfloat16 [32768, 256], P(('dp', 'section')), may hold values from -1 to 1, as said below
- owner: int32 [64], replicated, may hold values from 0 to 63, each once
- pointer: int32 [8], P('dp'), may hold values from 0 to 4088
Outputs:
- momentum_embeddings: bfloat16 [64, 256], P('dp')
- query_loss: float32 [64], P('dp')
- total_loss: float32 [], replicated
- new_queue: bfloat16 [32768, 256], P(('dp', 'section'))
Inputs may be any that keep to these rules, and one draw needn't show every extreme that they name: `queue`: every row has Euclidean norm below 1. Each value appears once: key j goes to group owner[j] // 8, so every group receives exactly 8 keys. `pointer`: first row of the group's shard where its new keys are written.
All inputs are finite; a program needn't handle non-finite values.
Results may differ from a plain program's by a relative error of at most 0.02.
Values may be sent and summed in bfloat16 or wider, within the bound.
No kernel may reach another device: no remote copies, remote signals or barrier semaphores. Data moves between devices by JAX's collectives and lax.ppermute only.
A program may use at most 128 MiB of HBM per device.

v0:
```python
import math
import jax
import jax.numpy as jnp
from jax import lax
from jax.sharding import PartitionSpec as P

HEADS = 16
HEAD_DIM = 64
TOKS = 197
IMG_MB = 2
contrastive_sharpness = 0.2


def from_behind(value, axis, steps):
    count = lax.axis_size(axis)
    initial, last = (max(0, -steps), min(count, count - steps))
    return lax.ppermute(value, axis, [(source, source + steps) for source in range(initial, last)])


def broadcast(value, axis, source):
    kept = jnp.where(lax.axis_index(axis) == source, value, 0).astype(value.dtype)
    return lax.psum(kept, axis)


def layer_norm(values, gain):
    center = values - jnp.mean(values, axis=-1, keepdims=True)
    spread = jnp.mean(center * center, axis=-1, keepdims=True)
    return center * lax.rsqrt(spread + 1e-06) * gain


def encoder_block(hidden, gain_one, qkv_weight, out_weight, gain_two, first_weight, second_weight):
    images = hidden.shape[0]
    width = hidden.shape[2]
    stream = hidden.astype(jnp.float32)
    normed = layer_norm(stream, gain_one).astype(jnp.bfloat16).reshape(images * TOKS, width)
    packed = jnp.dot(normed, qkv_weight, preferred_element_type=jnp.float32).astype(jnp.bfloat16)
    packed = packed.reshape(images, TOKS, 3, HEADS, HEAD_DIM)
    similarity_matrix = jnp.einsum(
        "bqhd,bkhd->bhqk", packed[:, :, 0], packed[:, :, 1], preferred_element_type=jnp.float32
    )
    similarity_matrix = similarity_matrix / math.sqrt(HEAD_DIM)
    peak = jnp.max(similarity_matrix, axis=-1, keepdims=True)
    expo = jnp.exp(similarity_matrix - peak)
    probs = (expo / jnp.sum(expo, axis=-1, keepdims=True)).astype(jnp.bfloat16)
    context = jnp.einsum(
        "bhqk,bkhd->bqhd", probs, packed[:, :, 2], preferred_element_type=jnp.float32
    )
    context = context.astype(jnp.bfloat16).reshape(images * TOKS, width)
    stream = stream + jnp.dot(context, out_weight, preferred_element_type=jnp.float32).reshape(
        images, TOKS, width
    )
    normed = layer_norm(stream, gain_two).astype(jnp.bfloat16).reshape(images * TOKS, width)
    inner = jax.nn.gelu(
        jnp.dot(normed, first_weight, preferred_element_type=jnp.float32), approximate=False
    )
    inner = inner.astype(jnp.bfloat16)
    stream = stream + jnp.dot(inner, second_weight, preferred_element_type=jnp.float32).reshape(
        images, TOKS, width
    )
    return stream.astype(jnp.bfloat16)


def key_head(class_rows, final_norm_gain, w_head):
    normed = layer_norm(class_rows.astype(jnp.float32), final_norm_gain).astype(jnp.bfloat16)
    projected = jnp.dot(normed, w_head, preferred_element_type=jnp.float32)
    scale = lax.rsqrt(1.0 + jnp.sum(projected * projected, axis=1, keepdims=True))
    return (projected * scale).astype(jnp.bfloat16)


def on_device(
    patches,
    ln1_gain,
    w_qkv,
    w_out,
    ln2_gain,
    w_fc1,
    w_fc2,
    final_norm_gain,
    w_head,
    online_embeddings,
    queue,
    owner,
    pointer,
):
    sections = lax.axis_size("section")
    section_index = lax.axis_index("section")
    group_index = lax.axis_index("dp")
    group_images = patches.shape[0]
    width = patches.shape[2]
    batch_size = IMG_MB // 2
    blocks = group_images // batch_size
    feeds = patches.reshape(blocks, batch_size, TOKS, width)

    def run_block(hidden):
        return encoder_block(
            hidden, ln1_gain[0], w_qkv[0], w_out[0], ln2_gain[0], w_fc1[0], w_fc2[0]
        )

    def keep_block(hidden):
        return hidden

    def advance(tick, carry):
        incoming, finished = carry
        fresh = lax.dynamic_index_in_dim(feeds, jnp.minimum(tick, blocks - 1), 0, keepdims=False)
        source = jnp.where(section_index == 0, fresh, incoming)
        active = jnp.logical_and(tick >= section_index, tick - section_index < blocks)
        result = lax.cond(active, run_block, keep_block, source)
        place = jnp.clip(tick - (sections - 1), 0, blocks - 1)
        stored = lax.dynamic_update_index_in_dim(finished, result[:, 0, :], place, 0)
        finished = jnp.where(tick >= sections - 1, stored, finished)
        passed = from_behind(result, "section", 1)
        return (passed, finished)

    start = (jnp.zeros_like(feeds[0]), jnp.zeros((blocks, batch_size, width), jnp.bfloat16))
    passed, finished = lax.fori_loop(0, blocks + sections - 1, advance, start)
    resident_embeddings = key_head(finished.reshape(group_images, width), final_norm_gain, w_head)
    momentum_embeddings = broadcast(resident_embeddings, "section", sections - 1)
    query_rows_full = lax.all_gather(online_embeddings, "dp", axis=0, tiled=True)
    share = queue.shape[0]
    similarity_matrix = (
        jnp.einsum("tw,fw->tf", query_rows_full, queue, preferred_element_type=jnp.float32)
        / contrastive_sharpness
    )
    local_peak = jnp.max(similarity_matrix, axis=1)
    top = lax.pmax(local_peak, ("dp", "section"))
    total = lax.psum(jnp.sum(jnp.exp(similarity_matrix - top[:, None]), axis=1), ("dp", "section"))
    negative_all = top + jnp.log(total)
    negative = lax.dynamic_slice_in_dim(negative_all, group_index * group_images, group_images, 0)
    matching_similarity = (
        jnp.sum(
            online_embeddings.astype(jnp.float32) * momentum_embeddings.astype(jnp.float32), axis=1
        )
        / contrastive_sharpness
    )
    larger = jnp.maximum(negative, matching_similarity)
    query_loss = (
        larger
        + jnp.log(jnp.exp(negative - larger) + jnp.exp(matching_similarity - larger))
        - matching_similarity
    )
    loss_sum = lax.psum(jnp.sum(query_loss), "dp")
    total_loss = loss_sum / (group_images * lax.axis_size("dp"))
    every_key = lax.all_gather(momentum_embeddings, "dp", axis=0, tiled=True)
    wanted = group_index * group_images + jnp.arange(group_images, dtype=jnp.int32)
    selector = (owner[None, :] == wanted[:, None]).astype(jnp.bfloat16)
    incoming_keys = jnp.dot(selector, every_key, preferred_element_type=jnp.float32).astype(
        jnp.bfloat16
    )
    row_place = section_index * share + jnp.arange(share, dtype=jnp.int32)
    slot_index = row_place - pointer[0]
    placing = (slot_index[:, None] == jnp.arange(group_images, dtype=jnp.int32)[None, :]).astype(
        jnp.bfloat16
    )
    written = jnp.dot(placing, incoming_keys, preferred_element_type=jnp.float32).astype(
        jnp.bfloat16
    )
    inside = jnp.logical_and(slot_index >= 0, slot_index < group_images)
    new_queue = jnp.where(inside[:, None], written, queue)
    return (momentum_embeddings, query_loss, total_loss, new_queue)


def solution(mesh):
    placed = (
        P("dp", None, None),
        P("section", None),
        P("section", None, None),
        P("section", None, None),
        P("section", None),
        P("section", None, None),
        P("section", None, None),
        P(),
        P(),
        P("dp", None),
        P(("dp", "section"), None),
        P(),
        P("dp"),
    )
    return jax.shard_map(
        on_device,
        mesh=mesh,
        in_specs=placed,
        out_specs=(P("dp", None), P("dp"), P(), P(("dp", "section"), None)),
        check_vma=False,
    )
```

profile of v0, /device:TPU:0, one launch (start us, length us, event | category | flops | bytes accessed | tf_op | source)
XLA Modules:
  0.0 522.6 jit_solution(10496831233054502232)
XLA Ops:
  6.2 320.3 %while.17 = (s32[]{:T(128)}, bf16[1,197,1024]{2,1,0:T(8,128)(2,1)S(1)}, bf16[8,1,1024]{2,1,0:T(2,128)(2,1)S(1)}, s32[]{:T(128)}, pred[]{:T(512)}, /*index=5*/bf1...) while((s32[]{:T(128)}, ...), condition=%wide.region_9.10_spmd, body=%wide.region_0.9_spmd.sunk | while | flops 3499673600 | bytes 49231128 | solution.py:115
  7.4 22.1 %conditional.2 = (bf16[1,197,1024]{2,1,0:T(8,128)(2,1)S(1)}) conditional(s32[]{:T(128)} %convert_element_type.128, bf16[1,197,1024]{2,1,0:T(8,128)(2,1)S(1)} %bitcast_select_fusion.2, (bf16[1,197,1024]{2,1,0:T(8,128)(2,1)S(1)}, f32[1,1024]{1,0:T(1,128)S(1)}, bf16[1,1024,3072]{2,1,0:T(8,128)(2,1)}, bf16[1,1024,1024]{2,1,0:T(8,128)(2,1)}, ...), branch_computations={%region_1.1_spmd, %region_2.8_spmd} | conditional | flops 3499470848 | bytes 46394252 | solution.py:107
  20.7 8.7 %fusion.40 = bf16[1,197,1024]{2,1,0:T(8,128)(2,1)S(1)} fusion(f32[1,197,1024]{2,1,0:T(8,128)S(1)} %get-tuple-element.344, bf16[1,2048,1024]{2,1,0:T(8,128)(2,1)} %get-tuple-element.295, bf16[1,1024,2048]{2,1,0:T(8,128)(2,1)} %get-tuple-element.294, f32[1024]{0:T(1024)S(1)} %bitcast.93, f32[197]{0:T(256)S(1)} %add_rsqrt_fusion, ...), kind=kOutput, calls=%fused_computation.40 | convolution fusion | flops 1679990784 | bytes 9604648 | tf_op jit(solution)/shard_map/while/body/eval_jaxpr/cond/branch_1_fun/dot_general | solution.py:57
  33.2 22.1 %conditional.2 = (bf16[1,197,1024]{2,1,0:T(8,128)(2,1)S(1)}) conditional(s32[]{:T(128)} %convert_element_type.128, bf16[1,197,1024]{2,1,0:T(8,128)(2,1)S(1)} %bitcast_select_fusion.2, (bf16[1,197,1024]{2,1,0:T(8,128)(2,1)S(1)}, f32[1,1024]{1,0:T(1,128)S(1)}, bf16[1,1024,3072]{2,1,0:T(8,128)(2,1)}, bf16[1,1024,1024]{2,1,0:T(8,128)(2,1)}, ...), branch_computations={%region_1.1_spmd, %region_2.8_spmd} | conditional | flops 3499470848 | bytes 46394252 | solution.py:107
  46.6 8.7 %fusion.40 = bf16[1,197,1024]{2,1,0:T(8,128)(2,1)S(1)} fusion(f32[1,197,1024]{2,1,0:T(8,128)S(1)} %get-tuple-element.344, bf16[1,2048,1024]{2,1,0:T(8,128)(2,1)} %get-tuple-element.295, bf16[1,1024,2048]{2,1,0:T(8,128)(2,1)} %get-tuple-element.294, f32[1024]{0:T(1024)S(1)} %bitcast.93, f32[197]{0:T(256)S(1)} %add_rsqrt_fusion, ...), kind=kOutput, calls=%fused_computation.40 | convolution fusion | flops 1679990784 | bytes 9604648 | tf_op jit(solution)/shard_map/while/body/eval_jaxpr/cond/branch_1_fun/dot_general | solution.py:57
  60.0 22.1 %conditional.2 = (bf16[1,197,1024]{2,1,0:T(8,128)(2,1)S(1)}) conditional(s32[]{:T(128)} %convert_element_type.128, bf16[1,197,1024]{2,1,0:T(8,128)(2,1)S(1)} %bitcast_select_fusion.2, (bf16[1,197,1024]{2,1,0:T(8,128)(2,1)S(1)}, f32[1,1024]{1,0:T(1,128)S(1)}, bf16[1,1024,3072]{2,1,0:T(8,128)(2,1)}, bf16[1,1024,1024]{2,1,0:T(8,128)(2,1)}, ...), branch_computations={%region_1.1_spmd, %region_2.8_spmd} | conditional | flops 3499470848 | bytes 46394252 | solution.py:107
  73.4 8.7 %fusion.40 = bf16[1,197,1024]{2,1,0:T(8,128)(2,1)S(1)} fusion(f32[1,197,1024]{2,1,0:T(8,128)S(1)} %get-tuple-element.344, bf16[1,2048,1024]{2,1,0:T(8,128)(2,1)} %get-tuple-element.295, bf16[1,1024,2048]{2,1,0:T(8,128)(2,1)} %get-tuple-element.294, f32[1024]{0:T(1024)S(1)} %bitcast.93, f32[197]{0:T(256)S(1)} %add_rsqrt_fusion, ...), kind=kOutput, calls=%fused_computation.40 | convolution fusion | flops 1679990784 | bytes 9604648 | tf_op jit(solution)/shard_map/while/body/eval_jaxpr/cond/branch_1_fun/dot_general | solution.py:57
  82.2 5.5 %collective-permute-start = (bf16[1,197,1024]{2,1,0:T(8,128)(2,1)S(1)}, bf16[1,197,1024]{2,1,0:T(8,128)(2,1)S(1)}, u32[]{:S(2)}, u32[]{:S(2)}) collective-permute-start(bf16[1,197,1024]{2,1,0:T(8,128)(2,1)S(1)} %get-tuple-element.476), channel_id=1, source_target_pairs={{0,1},{1,2},{2,3},{4,5},{5,6},{6,7},{8,9},{9,10},{10,11},{12,13},{... | collective-permute-start | bytes 1210376 | tf_op jit(solution)/shard_map/while/body/eval_jaxpr/ppermute | solution.py:17
  90.0 22.1 %conditional.2 = (bf16[1,197,1024]{2,1,0:T(8,128)(2,1)S(1)}) conditional(s32[]{:T(128)} %convert_element_type.128, bf16[1,197,1024]{2,1,0:T(8,128)(2,1)S(1)} %bitcast_select_fusion.2, (bf16[1,197,1024]{2,1,0:T(8,128)(2,1)S(1)}, f32[1,1024]{1,0:T(1,128)S(1)}, bf16[1,1024,3072]{2,1,0:T(8,128)(2,1)}, bf16[1,1024,1024]{2,1,0:T(8,128)(2,1)}, ...), branch_computations={%region_1.1_spmd, %region_2.8_spmd} | conditional | flops 3499470848 | bytes 46394252 | solution.py:107
  103.4 8.7 %fusion.40 = bf16[1,197,1024]{2,1,0:T(8,128)(2,1)S(1)} fusion(f32[1,197,1024]{2,1,0:T(8,128)S(1)} %get-tuple-element.344, bf16[1,2048,1024]{2,1,0:T(8,128)(2,1)} %get-tuple-element.295, bf16[1,1024,2048]{2,1,0:T(8,128)(2,1)} %get-tuple-element.294, f32[1024]{0:T(1024)S(1)} %bitcast.93, f32[197]{0:T(256)S(1)} %add_rsqrt_fusion, ...), kind=kOutput, calls=%fused_computation.40 | convolution fusion | flops 1679990784 | bytes 9604648 | tf_op jit(solution)/shard_map/while/body/eval_jaxpr/cond/branch_1_fun/dot_general | solution.py:57
  112.2 7.9 %collective-permute-start = (bf16[1,197,1024]{2,1,0:T(8,128)(2,1)S(1)}, bf16[1,197,1024]{2,1,0:T(8,128)(2,1)S(1)}, u32[]{:S(2)}, u32[]{:S(2)}) collective-permute-start(bf16[1,197,1024]{2,1,0:T(8,128)(2,1)S(1)} %get-tuple-element.476), channel_id=1, source_target_pairs={{0,1},{1,2},{2,3},{4,5},{5,6},{6,7},{8,9},{9,10},{10,11},{12,13},{... | collective-permute-start | bytes 1210376 | tf_op jit(solution)/shard_map/while/body/eval_jaxpr/ppermute | solution.py:17
  122.5 22.1 %conditional.2 = (bf16[1,197,1024]{2,1,0:T(8,128)(2,1)S(1)}) conditional(s32[]{:T(128)} %convert_element_type.128, bf16[1,197,1024]{2,1,0:T(8,128)(2,1)S(1)} %bitcast_select_fusion.2, (bf16[1,197,1024]{2,1,0:T(8,128)(2,1)S(1)}, f32[1,1024]{1,0:T(1,128)S(1)}, bf16[1,1024,3072]{2,1,0:T(8,128)(2,1)}, bf16[1,1024,1024]{2,1,0:T(8,128)(2,1)}, ...), branch_computations={%region_1.1_spmd, %region_2.8_spmd} | conditional | flops 3499470848 | bytes 46394252 | solution.py:107
  135.9 8.7 %fusion.40 = bf16[1,197,1024]{2,1,0:T(8,128)(2,1)S(1)} fusion(f32[1,197,1024]{2,1,0:T(8,128)S(1)} %get-tuple-element.344, bf16[1,2048,1024]{2,1,0:T(8,128)(2,1)} %get-tuple-element.295, bf16[1,1024,2048]{2,1,0:T(8,128)(2,1)} %get-tuple-element.294, f32[1024]{0:T(1024)S(1)} %bitcast.93, f32[197]{0:T(256)S(1)} %add_rsqrt_fusion, ...), kind=kOutput, calls=%fused_computation.40 | convolution fusion | flops 1679990784 | bytes 9604648 | tf_op jit(solution)/shard_map/while/body/eval_jaxpr/cond/branch_1_fun/dot_general | solution.py:57
  144.6 7.9 %collective-permute-start = (bf16[1,197,1024]{2,1,0:T(8,128)(2,1)S(1)}, bf16[1,197,1024]{2,1,0:T(8,128)(2,1)S(1)}, u32[]{:S(2)}, u32[]{:S(2)}) collective-permute-start(bf16[1,197,1024]{2,1,0:T(8,128)(2,1)S(1)} %get-tuple-element.476), channel_id=1, source_target_pairs={{0,1},{1,2},{2,3},{4,5},{5,6},{6,7},{8,9},{9,10},{10,11},{12,13},{... | collective-permute-start | bytes 1210376 | tf_op jit(solution)/shard_map/while/body/eval_jaxpr/ppermute | solution.py:17
  154.9 22.1 %conditional.2 = (bf16[1,197,1024]{2,1,0:T(8,128)(2,1)S(1)}) conditional(s32[]{:T(128)} %convert_element_type.128, bf16[1,197,1024]{2,1,0:T(8,128)(2,1)S(1)} %bitcast_select_fusion.2, (bf16[1,197,1024]{2,1,0:T(8,128)(2,1)S(1)}, f32[1,1024]{1,0:T(1,128)S(1)}, bf16[1,1024,3072]{2,1,0:T(8,128)(2,1)}, bf16[1,1024,1024]{2,1,0:T(8,128)(2,1)}, ...), branch_computations={%region_1.1_spmd, %region_2.8_spmd} | conditional | flops 3499470848 | bytes 46394252 | solution.py:107
  168.3 8.7 %fusion.40 = bf16[1,197,1024]{2,1,0:T(8,128)(2,1)S(1)} fusion(f32[1,197,1024]{2,1,0:T(8,128)S(1)} %get-tuple-element.344, bf16[1,2048,1024]{2,1,0:T(8,128)(2,1)} %get-tuple-element.295, bf16[1,1024,2048]{2,1,0:T(8,128)(2,1)} %get-tuple-element.294, f32[1024]{0:T(1024)S(1)} %bitcast.93, f32[197]{0:T(256)S(1)} %add_rsqrt_fusion, ...), kind=kOutput, calls=%fused_computation.40 | convolution fusion | flops 1679990784 | bytes 9604648 | tf_op jit(solution)/shard_map/while/body/eval_jaxpr/cond/branch_1_fun/dot_general | solution.py:57
  177.1 7.9 %collective-permute-start = (bf16[1,197,1024]{2,1,0:T(8,128)(2,1)S(1)}, bf16[1,197,1024]{2,1,0:T(8,128)(2,1)S(1)}, u32[]{:S(2)}, u32[]{:S(2)}) collective-permute-start(bf16[1,197,1024]{2,1,0:T(8,128)(2,1)S(1)} %get-tuple-element.476), channel_id=1, source_target_pairs={{0,1},{1,2},{2,3},{4,5},{5,6},{6,7},{8,9},{9,10},{10,11},{12,13},{... | collective-permute-start | bytes 1210376 | tf_op jit(solution)/shard_map/while/body/eval_jaxpr/ppermute | solution.py:17
  187.4 22.1 %conditional.2 = (bf16[1,197,1024]{2,1,0:T(8,128)(2,1)S(1)}) conditional(s32[]{:T(128)} %convert_element_type.128, bf16[1,197,1024]{2,1,0:T(8,128)(2,1)S(1)} %bitcast_select_fusion.2, (bf16[1,197,1024]{2,1,0:T(8,128)(2,1)S(1)}, f32[1,1024]{1,0:T(1,128)S(1)}, bf16[1,1024,3072]{2,1,0:T(8,128)(2,1)}, bf16[1,1024,1024]{2,1,0:T(8,128)(2,1)}, ...), branch_computations={%region_1.1_spmd, %region_2.8_spmd} | conditional | flops 3499470848 | bytes 46394252 | solution.py:107
  200.8 8.7 %fusion.40 = bf16[1,197,1024]{2,1,0:T(8,128)(2,1)S(1)} fusion(f32[1,197,1024]{2,1,0:T(8,128)S(1)} %get-tuple-element.344, bf16[1,2048,1024]{2,1,0:T(8,128)(2,1)} %get-tuple-element.295, bf16[1,1024,2048]{2,1,0:T(8,128)(2,1)} %get-tuple-element.294, f32[1024]{0:T(1024)S(1)} %bitcast.93, f32[197]{0:T(256)S(1)} %add_rsqrt_fusion, ...), kind=kOutput, calls=%fused_computation.40 | convolution fusion | flops 1679990784 | bytes 9604648 | tf_op jit(solution)/shard_map/while/body/eval_jaxpr/cond/branch_1_fun/dot_general | solution.py:57
  209.5 7.9 %collective-permute-start = (bf16[1,197,1024]{2,1,0:T(8,128)(2,1)S(1)}, bf16[1,197,1024]{2,1,0:T(8,128)(2,1)S(1)}, u32[]{:S(2)}, u32[]{:S(2)}) collective-permute-start(bf16[1,197,1024]{2,1,0:T(8,128)(2,1)S(1)} %get-tuple-element.476), channel_id=1, source_target_pairs={{0,1},{1,2},{2,3},{4,5},{5,6},{6,7},{8,9},{9,10},{10,11},{12,13},{... | collective-permute-start | bytes 1210376 | tf_op jit(solution)/shard_map/while/body/eval_jaxpr/ppermute | solution.py:17
  219.8 22.1 %conditional.2 = (bf16[1,197,1024]{2,1,0:T(8,128)(2,1)S(1)}) conditional(s32[]{:T(128)} %convert_element_type.128, bf16[1,197,1024]{2,1,0:T(8,128)(2,1)S(1)} %bitcast_select_fusion.2, (bf16[1,197,1024]{2,1,0:T(8,128)(2,1)S(1)}, f32[1,1024]{1,0:T(1,128)S(1)}, bf16[1,1024,3072]{2,1,0:T(8,128)(2,1)}, bf16[1,1024,1024]{2,1,0:T(8,128)(2,1)}, ...), branch_computations={%region_1.1_spmd, %region_2.8_spmd} | conditional | flops 3499470848 | bytes 46394252 | solution.py:107
  233.2 8.7 %fusion.40 = bf16[1,197,1024]{2,1,0:T(8,128)(2,1)S(1)} fusion(f32[1,197,1024]{2,1,0:T(8,128)S(1)} %get-tuple-element.344, bf16[1,2048,1024]{2,1,0:T(8,128)(2,1)} %get-tuple-element.295, bf16[1,1024,2048]{2,1,0:T(8,128)(2,1)} %get-tuple-element.294, f32[1024]{0:T(1024)S(1)} %bitcast.93, f32[197]{0:T(256)S(1)} %add_rsqrt_fusion, ...), kind=kOutput, calls=%fused_computation.40 | convolution fusion | flops 1679990784 | bytes 9604648 | tf_op jit(solution)/shard_map/while/body/eval_jaxpr/cond/branch_1_fun/dot_general | solution.py:57
  242.0 7.9 %collective-permute-start = (bf16[1,197,1024]{2,1,0:T(8,128)(2,1)S(1)}, bf16[1,197,1024]{2,1,0:T(8,128)(2,1)S(1)}, u32[]{:S(2)}, u32[]{:S(2)}) collective-permute-start(bf16[1,197,1024]{2,1,0:T(8,128)(2,1)S(1)} %get-tuple-element.476), channel_id=1, source_target_pairs={{0,1},{1,2},{2,3},{4,5},{5,6},{6,7},{8,9},{9,10},{10,11},{12,13},{... | collective-permute-start | bytes 1210376 | tf_op jit(solution)/shard_map/while/body/eval_jaxpr/ppermute | solution.py:17
  252.3 30.1 %collective-permute-start = (bf16[1,197,1024]{2,1,0:T(8,128)(2,1)S(1)}, bf16[1,197,1024]{2,1,0:T(8,128)(2,1)S(1)}, u32[]{:S(2)}, u32[]{:S(2)}) collective-permute-start(bf16[1,197,1024]{2,1,0:T(8,128)(2,1)S(1)} %get-tuple-element.476), channel_id=1, source_target_pairs={{0,1},{1,2},{2,3},{4,5},{5,6},{6,7},{8,9},{9,10},{10,11},{12,13},{... | collective-permute-start | bytes 1210376 | tf_op jit(solution)/shard_map/while/body/eval_jaxpr/ppermute | solution.py:17
  284.8 7.9 %collective-permute-start = (bf16[1,197,1024]{2,1,0:T(8,128)(2,1)S(1)}, bf16[1,197,1024]{2,1,0:T(8,128)(2,1)S(1)}, u32[]{:S(2)}, u32[]{:S(2)}) collective-permute-start(bf16[1,197,1024]{2,1,0:T(8,128)(2,1)S(1)} %get-tuple-element.476), channel_id=1, source_target_pairs={{0,1},{1,2},{2,3},{4,5},{5,6},{6,7},{8,9},{9,10},{10,11},{12,13},{... | collective-permute-start | bytes 1210376 | tf_op jit(solution)/shard_map/while/body/eval_jaxpr/ppermute | solution.py:17
  295.1 30.1 %collective-permute-start = (bf16[1,197,1024]{2,1,0:T(8,128)(2,1)S(1)}, bf16[1,197,1024]{2,1,0:T(8,128)(2,1)S(1)}, u32[]{:S(2)}, u32[]{:S(2)}) collective-permute-start(bf16[1,197,1024]{2,1,0:T(8,128)(2,1)S(1)} %get-tuple-element.476), channel_id=1, source_target_pairs={{0,1},{1,2},{2,3},{4,5},{5,6},{6,7},{8,9},{9,10},{10,11},{12,13},{... | collective-permute-start | bytes 1210376 | tf_op jit(solution)/shard_map/while/body/eval_jaxpr/ppermute | solution.py:17
  327.3 24.5 %psum.21 = bf16[8,256]{1,0:T(8,128)(2,1)S(1)} all-reduce(bf16[8,256]{1,0:T(8,128)(2,1)S(1)} %fusion.136), channel_id=1, replica_groups=mesh['dp'=8,'section'=4] {'section'}, use_global_device_ids=true, to_apply=%region_13.14 | all-reduce | flops 2048 | bytes 8192 | tf_op jit(solution)/shard_map/psum | solution.py:22
  351.8 32.6 %all_gather.7 = bf16[64,256]{1,0:T(8,128)(2,1)S(1)} all-gather(bf16[8,256]{1,0:T(8,128)(2,1)S(1)} %psum.21), channel_id=1, replica_groups=mesh['dp'=8,'section'=4] {'dp'}, dimensions={0}, use_global_device_ids=true | all-gather | bytes 36864 | tf_op jit(solution)/shard_map/all_gather | solution.py:143
  386.5 30.6 %all_gather.6 = bf16[64,256]{1,0:T(8,128)(2,1)S(1)} all-gather(bf16[8,256]{1,0:T(8,128)(2,1)S(1)} %copy-done.4), channel_id=1, replica_groups=mesh['dp'=8,'section'=4] {'dp'}, dimensions={0}, use_global_device_ids=true | all-gather | bytes 36864 | tf_op jit(solution)/shard_map/all_gather | solution.py:118
  417.5 38.5 %pmax.7 = f32[64]{0:T(128)S(1)} all-reduce(f32[64]{0:T(128)S(1)} %get-tuple-element.347), channel_id=1, replica_groups=mesh['dp'=8,'section'=4] {'dp','section'}, use_global_device_ids=true, to_apply=%region_15.16 | all-reduce | flops 64 | bytes 512 | tf_op jit(solution)/shard_map/pmax | solution.py:125
  456.3 41.6 %psum.22 = f32[64]{0:T(128)S(1)} all-reduce(f32[64]{0:T(128)S(1)} %exponential_reduce_fusion), channel_id=1, replica_groups=mesh['dp'=8,'section'=4] {'dp','section'}, use_global_device_ids=true, to_apply=%region_17.18 | all-reduce | flops 64 | bytes 512 | tf_op jit(solution)/shard_map/psum | solution.py:126
  499.1 21.7 %psum.23 = f32[]{:T(128)} all-reduce(f32[]{:T(128)} %get-tuple-element.339), channel_id=1, replica_groups=mesh['dp'=8,'section'=4] {'dp'}, use_global_device_ids=true, to_apply=%region_20.21 | all-reduce | flops 1 | bytes 8 | tf_op jit(solution)/shard_map/psum | solution.py:141
  (194 shorter events, 145.8 us)
Async XLA Ops:
  0.6 326.3 %copy-start = (bf16[1024,256]{1,0:T(8,128)(2,1)S(1)}, bf16[1024,256]{1,0:T(8,128)(2,1)}, u32[]{:S(2)}) copy-start(bf16[1024,256]{1,0:T(8,128)(2,1)} %param.25) | copy-start | bytes 1572868
  0.7 5.5 %copy-start.6 = (f32[1,1024]{1,0:T(1,128)S(1)}, f32[1,1024]{1,0:T(1,128)}, u32[]{:S(2)}) copy-start(f32[1,1024]{1,0:T(1,128)} %param.18) | copy-start | bytes 12292
  0.7 5.5 %copy-start.7 = (f32[1,1024]{1,0:T(1,128)S(1)}, f32[1,1024]{1,0:T(1,128)}, u32[]{:S(2)}) copy-start(f32[1,1024]{1,0:T(1,128)} %param.21) | copy-start | bytes 12292
  6.2 320.7 %copy-start.8 = (f32[1024]{0:T(1024)S(1)}, f32[1024]{0:T(1024)}, u32[]{:S(2)}) copy-start(f32[1024]{0:T(1024)} %param.24) | copy-start | bytes 12292
  6.2 378.9 %copy-start.2 = (bf16[1024,256]{1,0:T(8,128)(2,1)S(1)}, bf16[1024,256]{1,0:T(8,128)(2,1)}, u32[]{:S(2)}) copy-start(bf16[1024,256]{1,0:T(8,128)(2,1)} %param.27) | copy-start | bytes 1572868
  6.2 378.9 %copy-start.5 = (s32[64]{0:T(128)S(1)}, s32[64]{0:T(128)}, u32[]{:S(2)}) copy-start(s32[64]{0:T(128)} %param.28) | copy-start | bytes 772
  18.2 1.6 copy-start.1
  29.5 2.7 collective-permute-start
  44.0 1.6 copy-start.1
  55.3 3.7 collective-permute-start
  70.9 1.6 copy-start.1
  82.2 6.8 %collective-permute-start = (bf16[1,197,1024]{2,1,0:T(8,128)(2,1)S(1)}, bf16[1,197,1024]{2,1,0:T(8,128)(2,1)S(1)}, u32[]{:S(2)}, u32[]{:S(2)}) collective-permute-start(bf16[1,197,1024]{2,1,0:T(8,128)(2,1)S(1)} %get-tuple-element.476), channel_id=1, source_target_pairs={{0,1},{1,2},{2,3},{4,5},{5,6},{6,7},{8,9},{9,10},{10,11},{12,13},{... | collective-permute-start | bytes 1210376 | tf_op jit(solution)/shard_map/while/body/eval_jaxpr/ppermute | solution.py:17
  100.9 1.6 copy-start.1
  112.2 9.3 %collective-permute-start = (bf16[1,197,1024]{2,1,0:T(8,128)(2,1)S(1)}, bf16[1,197,1024]{2,1,0:T(8,128)(2,1)S(1)}, u32[]{:S(2)}, u32[]{:S(2)}) collective-permute-start(bf16[1,197,1024]{2,1,0:T(8,128)(2,1)S(1)} %get-tuple-element.476), channel_id=1, source_target_pairs={{0,1},{1,2},{2,3},{4,5},{5,6},{6,7},{8,9},{9,10},{10,11},{12,13},{... | collective-permute-start | bytes 1210376 | tf_op jit(solution)/shard_map/while/body/eval_jaxpr/ppermute | solution.py:17
  133.3 1.6 copy-start.1
  144.6 9.3 %collective-permute-start = (bf16[1,197,1024]{2,1,0:T(8,128)(2,1)S(1)}, bf16[1,197,1024]{2,1,0:T(8,128)(2,1)S(1)}, u32[]{:S(2)}, u32[]{:S(2)}) collective-permute-start(bf16[1,197,1024]{2,1,0:T(8,128)(2,1)S(1)} %get-tuple-element.476), channel_id=1, source_target_pairs={{0,1},{1,2},{2,3},{4,5},{5,6},{6,7},{8,9},{9,10},{10,11},{12,13},{... | collective-permute-start | bytes 1210376 | tf_op jit(solution)/shard_map/while/body/eval_jaxpr/ppermute | solution.py:17
  165.8 1.6 copy-start.1
  177.1 9.3 %collective-permute-start = (bf16[1,197,1024]{2,1,0:T(8,128)(2,1)S(1)}, bf16[1,197,1024]{2,1,0:T(8,128)(2,1)S(1)}, u32[]{:S(2)}, u32[]{:S(2)}) collective-permute-start(bf16[1,197,1024]{2,1,0:T(8,128)(2,1)S(1)} %get-tuple-element.476), channel_id=1, source_target_pairs={{0,1},{1,2},{2,3},{4,5},{5,6},{6,7},{8,9},{9,10},{10,11},{12,13},{... | collective-permute-start | bytes 1210376 | tf_op jit(solution)/shard_map/while/body/eval_jaxpr/ppermute | solution.py:17
  198.2 1.6 copy-start.1
  209.5 9.3 %collective-permute-start = (bf16[1,197,1024]{2,1,0:T(8,128)(2,1)S(1)}, bf16[1,197,1024]{2,1,0:T(8,128)(2,1)S(1)}, u32[]{:S(2)}, u32[]{:S(2)}) collective-permute-start(bf16[1,197,1024]{2,1,0:T(8,128)(2,1)S(1)} %get-tuple-element.476), channel_id=1, source_target_pairs={{0,1},{1,2},{2,3},{4,5},{5,6},{6,7},{8,9},{9,10},{10,11},{12,13},{... | collective-permute-start | bytes 1210376 | tf_op jit(solution)/shard_map/while/body/eval_jaxpr/ppermute | solution.py:17
  230.7 1.6 copy-start.1
  242.0 9.3 %collective-permute-start = (bf16[1,197,1024]{2,1,0:T(8,128)(2,1)S(1)}, bf16[1,197,1024]{2,1,0:T(8,128)(2,1)S(1)}, u32[]{:S(2)}, u32[]{:S(2)}) collective-permute-start(bf16[1,197,1024]{2,1,0:T(8,128)(2,1)S(1)} %get-tuple-element.476), channel_id=1, source_target_pairs={{0,1},{1,2},{2,3},{4,5},{5,6},{6,7},{8,9},{9,10},{10,11},{12,13},{... | collective-permute-start | bytes 1210376 | tf_op jit(solution)/shard_map/while/body/eval_jaxpr/ppermute | solution.py:17
  252.3 31.4 %collective-permute-start = (bf16[1,197,1024]{2,1,0:T(8,128)(2,1)S(1)}, bf16[1,197,1024]{2,1,0:T(8,128)(2,1)S(1)}, u32[]{:S(2)}, u32[]{:S(2)}) collective-permute-start(bf16[1,197,1024]{2,1,0:T(8,128)(2,1)S(1)} %get-tuple-element.476), channel_id=1, source_target_pairs={{0,1},{1,2},{2,3},{4,5},{5,6},{6,7},{8,9},{9,10},{10,11},{12,13},{... | collective-permute-start | bytes 1210376 | tf_op jit(solution)/shard_map/while/body/eval_jaxpr/ppermute | solution.py:17
  284.8 9.3 %collective-permute-start = (bf16[1,197,1024]{2,1,0:T(8,128)(2,1)S(1)}, bf16[1,197,1024]{2,1,0:T(8,128)(2,1)S(1)}, u32[]{:S(2)}, u32[]{:S(2)}) collective-permute-start(bf16[1,197,1024]{2,1,0:T(8,128)(2,1)S(1)} %get-tuple-element.476), channel_id=1, source_target_pairs={{0,1},{1,2},{2,3},{4,5},{5,6},{6,7},{8,9},{9,10},{10,11},{12,13},{... | collective-permute-start | bytes 1210376 | tf_op jit(solution)/shard_map/while/body/eval_jaxpr/ppermute | solution.py:17
  295.1 31.4 %collective-permute-start = (bf16[1,197,1024]{2,1,0:T(8,128)(2,1)S(1)}, bf16[1,197,1024]{2,1,0:T(8,128)(2,1)S(1)}, u32[]{:S(2)}, u32[]{:S(2)}) collective-permute-start(bf16[1,197,1024]{2,1,0:T(8,128)(2,1)S(1)} %get-tuple-element.476), channel_id=1, source_target_pairs={{0,1},{1,2},{2,3},{4,5},{5,6},{6,7},{8,9},{9,10},{10,11},{12,13},{... | collective-permute-start | bytes 1210376 | tf_op jit(solution)/shard_map/while/body/eval_jaxpr/ppermute | solution.py:17
  326.5 59.9 %copy-start.4 = (bf16[8,256]{1,0:T(8,128)(2,1)S(1)}, bf16[8,256]{1,0:T(8,128)(2,1)}, u32[]{:S(2)}) copy-start(bf16[8,256]{1,0:T(8,128)(2,1)} %param.26) | copy-start | bytes 12292
  351.8 169.6 %copy-start.3 = (bf16[8,256]{1,0:T(8,128)(2,1)}, bf16[8,256]{1,0:T(8,128)(2,1)S(1)}, u32[]{:S(2)}) copy-start(bf16[8,256]{1,0:T(8,128)(2,1)S(1)} %psum.21) | copy-start | bytes 12292
where the time goes:
time: 524 us; the launch traced here: 523 us
  blocking collectives  190 us (36%)
  matrix products  130 us (25%)
  starting transfers between devices  117 us (22%)
  other arithmetic  40.6 us (8%)
  local copies, waits for them, and re-layouts  27.6 us (5%)
  waiting for transfers between devices  14.3 us (3%)
    ppermute x11, starting transfers between devices, from_behind(): lax.ppermute(value, axis, [(source, source + steps) for source in range(i...  117 us
    dot_general x8, matrix products, encoder_block(): jnp.dot(inner, second_weight, preferred_element_type=jnp.float32)  70 us
    dot_general x8, matrix products, encoder_block(): jnp.dot(normed, qkv_weight, preferred_element_type=jnp.float32)  43.2 us
    psum x1, blocking collectives, on_device(): lax.psum(jnp.sum(jnp.exp(similarity_matrix - top[:, None]), axis=1), ('dp...  41.6 us
    pmax x1, blocking collectives, on_device(): top = lax.pmax(local_peak, ('dp', 'section'))  38.5 us
    all_gather x1, blocking collectives, on_device(): every_key = lax.all_gather(momentum_embeddings, 'dp', axis=0, tiled=True)  32.6 us
    all_gather x1, blocking collectives, on_device(): lax.all_gather(online_embeddings, 'dp', axis=0, tiled=True)  30.6 us
    psum x1, blocking collectives, broadcast(): return lax.psum(kept, axis)  24.5 us
  transfers between devices with their start and end apart: 11, of which 11 were waited for; matrix products, arithmetic and copies ran while one was open for 0% of the time, Pallas kernels for 0%

commit v1 on v0

--- a/solution.py
+++ b/solution.py
@@ -123,7 +123,9 @@
     )
     local_peak = jnp.max(similarity_matrix, axis=1)
     top = lax.pmax(local_peak, ("dp", "section"))
-    total = lax.psum(jnp.sum(jnp.exp(similarity_matrix - top[:, None]), axis=1), ("dp", "section"))
+    total = lax.psum(
+        lax.psum(jnp.sum(jnp.exp(similarity_matrix - top[:, None]), axis=1), "section"), "dp"
+    )
     negative_all = top + jnp.log(total)
     negative = lax.dynamic_slice_in_dim(negative_all, group_index * group_images, group_images, 0)
     matching_similarity = (

time: 524 us -> 505 us (0.964)
  blocking collectives: 190 us -> 170 us
    psum x1 -> x2, blocking collectives: 41.6 us -> 26 us  [the longest x1 19.4 us: on_device(): lax.psum(lax.psum(jnp.sum(jnp.exp(similarity_matrix - top[:, None]), axis...]
where the time goes in v1:
time: 505 us; the launch traced here: 503 us
  blocking collectives  170 us (34%)
  matrix products  130 us (26%)
  starting transfers between devices  117 us (23%)
  other arithmetic  40.6 us (8%)
  local copies, waits for them, and re-layouts  27.6 us (5%)
  waiting for transfers between devices  14.3 us (3%)
    ppermute x11, starting transfers between devices, from_behind(): lax.ppermute(value, axis, [(source, source + steps) for source in range(i...  117 us
    dot_general x8, matrix products, encoder_block(): jnp.dot(inner, second_weight, preferred_element_type=jnp.float32)  70 us
    dot_general x8, matrix products, encoder_block(): jnp.dot(normed, qkv_weight, preferred_element_type=jnp.float32)  43.2 us
    pmax x1, blocking collectives, on_device(): top = lax.pmax(local_peak, ('dp', 'section'))  38.5 us
    all_gather x1, blocking collectives, on_device(): every_key = lax.all_gather(momentum_embeddings, 'dp', axis=0, tiled=True)  32.4 us
    all_gather x1, blocking collectives, on_device(): lax.all_gather(online_embeddings, 'dp', axis=0, tiled=True)  30.6 us
    psum x1, blocking collectives, broadcast(): return lax.psum(kept, axis)  24.5 us
    sub x8, other arithmetic, encoder_block(): expo = jnp.exp(similarity_matrix - peak)  21.6 us
  transfers between devices with their start and end apart: 11, of which 11 were waited for; matrix products, arithmetic and copies ran while one was open for 0% of the time, Pallas kernels for 0%

profile of v1, /device:TPU:0, one launch (start us, length us, event | category | flops | bytes accessed | tf_op | source)
XLA Modules:
  0.0 502.8 jit_solution(5158841526508921717)
XLA Ops:
  6.2 320.3 %while.17 = (s32[]{:T(128)}, bf16[1,197,1024]{2,1,0:T(8,128)(2,1)S(1)}, bf16[8,1,1024]{2,1,0:T(2,128)(2,1)S(1)}, s32[]{:T(128)}, pred[]{:T(512)}, /*index=5*/bf1...) while((s32[]{:T(128)}, ...), condition=%wide.region_9.10_spmd, body=%wide.region_0.9_spmd.sunk | while | flops 3499673600 | bytes 49231128 | solution.py:115
  7.4 22.1 %conditional.2 = (bf16[1,197,1024]{2,1,0:T(8,128)(2,1)S(1)}) conditional(s32[]{:T(128)} %convert_element_type.128, bf16[1,197,1024]{2,1,0:T(8,128)(2,1)S(1)} %bitcast_select_fusion.2, (bf16[1,197,1024]{2,1,0:T(8,128)(2,1)S(1)}, f32[1,1024]{1,0:T(1,128)S(1)}, bf16[1,1024,3072]{2,1,0:T(8,128)(2,1)}, bf16[1,1024,1024]{2,1,0:T(8,128)(2,1)}, ...), branch_computations={%region_1.1_spmd, %region_2.8_spmd} | conditional | flops 3499470848 | bytes 46394252 | solution.py:107
  20.7 8.7 %fusion.40 = bf16[1,197,1024]{2,1,0:T(8,128)(2,1)S(1)} fusion(f32[1,197,1024]{2,1,0:T(8,128)S(1)} %get-tuple-element.344, bf16[1,2048,1024]{2,1,0:T(8,128)(2,1)} %get-tuple-element.295, bf16[1,1024,2048]{2,1,0:T(8,128)(2,1)} %get-tuple-element.294, f32[1024]{0:T(1024)S(1)} %bitcast.93, f32[197]{0:T(256)S(1)} %add_rsqrt_fusion, ...), kind=kOutput, calls=%fused_computation.40 | convolution fusion | flops 1679990784 | bytes 9604648 | tf_op jit(solution)/shard_map/while/body/eval_jaxpr/cond/branch_1_fun/dot_general | solution.py:57
  33.2 22.1 %conditional.2 = (bf16[1,197,1024]{2,1,0:T(8,128)(2,1)S(1)}) conditional(s32[]{:T(128)} %convert_element_type.128, bf16[1,197,1024]{2,1,0:T(8,128)(2,1)S(1)} %bitcast_select_fusion.2, (bf16[1,197,1024]{2,1,0:T(8,128)(2,1)S(1)}, f32[1,1024]{1,0:T(1,128)S(1)}, bf16[1,1024,3072]{2,1,0:T(8,128)(2,1)}, bf16[1,1024,1024]{2,1,0:T(8,128)(2,1)}, ...), branch_computations={%region_1.1_spmd, %region_2.8_spmd} | conditional | flops 3499470848 | bytes 46394252 | solution.py:107
  46.6 8.7 %fusion.40 = bf16[1,197,1024]{2,1,0:T(8,128)(2,1)S(1)} fusion(f32[1,197,1024]{2,1,0:T(8,128)S(1)} %get-tuple-element.344, bf16[1,2048,1024]{2,1,0:T(8,128)(2,1)} %get-tuple-element.295, bf16[1,1024,2048]{2,1,0:T(8,128)(2,1)} %get-tuple-element.294, f32[1024]{0:T(1024)S(1)} %bitcast.93, f32[197]{0:T(256)S(1)} %add_rsqrt_fusion, ...), kind=kOutput, calls=%fused_computation.40 | convolution fusion | flops 1679990784 | bytes 9604648 | tf_op jit(solution)/shard_map/while/body/eval_jaxpr/cond/branch_1_fun/dot_general | solution.py:57
  60.0 22.1 %conditional.2 = (bf16[1,197,1024]{2,1,0:T(8,128)(2,1)S(1)}) conditional(s32[]{:T(128)} %convert_element_type.128, bf16[1,197,1024]{2,1,0:T(8,128)(2,1)S(1)} %bitcast_select_fusion.2, (bf16[1,197,1024]{2,1,0:T(8,128)(2,1)S(1)}, f32[1,1024]{1,0:T(1,128)S(1)}, bf16[1,1024,3072]{2,1,0:T(8,128)(2,1)}, bf16[1,1024,1024]{2,1,0:T(8,128)(2,1)}, ...), branch_computations={%region_1.1_spmd, %region_2.8_spmd} | conditional | flops 3499470848 | bytes 46394252 | solution.py:107
  73.4 8.7 %fusion.40 = bf16[1,197,1024]{2,1,0:T(8,128)(2,1)S(1)} fusion(f32[1,197,1024]{2,1,0:T(8,128)S(1)} %get-tuple-element.344, bf16[1,2048,1024]{2,1,0:T(8,128)(2,1)} %get-tuple-element.295, bf16[1,1024,2048]{2,1,0:T(8,128)(2,1)} %get-tuple-element.294, f32[1024]{0:T(1024)S(1)} %bitcast.93, f32[197]{0:T(256)S(1)} %add_rsqrt_fusion, ...), kind=kOutput, calls=%fused_computation.40 | convolution fusion | flops 1679990784 | bytes 9604648 | tf_op jit(solution)/shard_map/while/body/eval_jaxpr/cond/branch_1_fun/dot_general | solution.py:57
  90.0 22.1 %conditional.2 = (bf16[1,197,1024]{2,1,0:T(8,128)(2,1)S(1)}) conditional(s32[]{:T(128)} %convert_element_type.128, bf16[1,197,1024]{2,1,0:T(8,128)(2,1)S(1)} %bitcast_select_fusion.2, (bf16[1,197,1024]{2,1,0:T(8,128)(2,1)S(1)}, f32[1,1024]{1,0:T(1,128)S(1)}, bf16[1,1024,3072]{2,1,0:T(8,128)(2,1)}, bf16[1,1024,1024]{2,1,0:T(8,128)(2,1)}, ...), branch_computations={%region_1.1_spmd, %region_2.8_spmd} | conditional | flops 3499470848 | bytes 46394252 | solution.py:107
  103.4 8.7 %fusion.40 = bf16[1,197,1024]{2,1,0:T(8,128)(2,1)S(1)} fusion(f32[1,197,1024]{2,1,0:T(8,128)S(1)} %get-tuple-element.344, bf16[1,2048,1024]{2,1,0:T(8,128)(2,1)} %get-tuple-element.295, bf16[1,1024,2048]{2,1,0:T(8,128)(2,1)} %get-tuple-element.294, f32[1024]{0:T(1024)S(1)} %bitcast.93, f32[197]{0:T(256)S(1)} %add_rsqrt_fusion, ...), kind=kOutput, calls=%fused_computation.40 | convolution fusion | flops 1679990784 | bytes 9604648 | tf_op jit(solution)/shard_map/while/body/eval_jaxpr/cond/branch_1_fun/dot_general | solution.py:57
  112.2 7.9 %collective-permute-start = (bf16[1,197,1024]{2,1,0:T(8,128)(2,1)S(1)}, bf16[1,197,1024]{2,1,0:T(8,128)(2,1)S(1)}, u32[]{:S(2)}, u32[]{:S(2)}) collective-permute-start(bf16[1,197,1024]{2,1,0:T(8,128)(2,1)S(1)} %get-tuple-element.476), channel_id=1, source_target_pairs={{0,1},{1,2},{2,3},{4,5},{5,6},{6,7},{8,9},{9,10},{10,11},{12,13},{... | collective-permute-start | bytes 1210376 | tf_op jit(solution)/shard_map/while/body/eval_jaxpr/ppermute | solution.py:17
  122.5 22.1 %conditional.2 = (bf16[1,197,1024]{2,1,0:T(8,128)(2,1)S(1)}) conditional(s32[]{:T(128)} %convert_element_type.128, bf16[1,197,1024]{2,1,0:T(8,128)(2,1)S(1)} %bitcast_select_fusion.2, (bf16[1,197,1024]{2,1,0:T(8,128)(2,1)S(1)}, f32[1,1024]{1,0:T(1,128)S(1)}, bf16[1,1024,3072]{2,1,0:T(8,128)(2,1)}, bf16[1,1024,1024]{2,1,0:T(8,128)(2,1)}, ...), branch_computations={%region_1.1_spmd, %region_2.8_spmd} | conditional | flops 3499470848 | bytes 46394252 | solution.py:107
  135.9 8.7 %fusion.40 = bf16[1,197,1024]{2,1,0:T(8,128)(2,1)S(1)} fusion(f32[1,197,1024]{2,1,0:T(8,128)S(1)} %get-tuple-element.344, bf16[1,2048,1024]{2,1,0:T(8,128)(2,1)} %get-tuple-element.295, bf16[1,1024,2048]{2,1,0:T(8,128)(2,1)} %get-tuple-element.294, f32[1024]{0:T(1024)S(1)} %bitcast.93, f32[197]{0:T(256)S(1)} %add_rsqrt_fusion, ...), kind=kOutput, calls=%fused_computation.40 | convolution fusion | flops 1679990784 | bytes 9604648 | tf_op jit(solution)/shard_map/while/body/eval_jaxpr/cond/branch_1_fun/dot_general | solution.py:57
  144.6 7.9 %collective-permute-start = (bf16[1,197,1024]{2,1,0:T(8,128)(2,1)S(1)}, bf16[1,197,1024]{2,1,0:T(8,128)(2,1)S(1)}, u32[]{:S(2)}, u32[]{:S(2)}) collective-permute-start(bf16[1,197,1024]{2,1,0:T(8,128)(2,1)S(1)} %get-tuple-element.476), channel_id=1, source_target_pairs={{0,1},{1,2},{2,3},{4,5},{5,6},{6,7},{8,9},{9,10},{10,11},{12,13},{... | collective-permute-start | bytes 1210376 | tf_op jit(solution)/shard_map/while/body/eval_jaxpr/ppermute | solution.py:17
  154.9 22.1 %conditional.2 = (bf16[1,197,1024]{2,1,0:T(8,128)(2,1)S(1)}) conditional(s32[]{:T(128)} %convert_element_type.128, bf16[1,197,1024]{2,1,0:T(8,128)(2,1)S(1)} %bitcast_select_fusion.2, (bf16[1,197,1024]{2,1,0:T(8,128)(2,1)S(1)}, f32[1,1024]{1,0:T(1,128)S(1)}, bf16[1,1024,3072]{2,1,0:T(8,128)(2,1)}, bf16[1,1024,1024]{2,1,0:T(8,128)(2,1)}, ...), branch_computations={%region_1.1_spmd, %region_2.8_spmd} | conditional | flops 3499470848 | bytes 46394252 | solution.py:107
  168.3 8.7 %fusion.40 = bf16[1,197,1024]{2,1,0:T(8,128)(2,1)S(1)} fusion(f32[1,197,1024]{2,1,0:T(8,128)S(1)} %get-tuple-element.344, bf16[1,2048,1024]{2,1,0:T(8,128)(2,1)} %get-tuple-element.295, bf16[1,1024,2048]{2,1,0:T(8,128)(2,1)} %get-tuple-element.294, f32[1024]{0:T(1024)S(1)} %bitcast.93, f32[197]{0:T(256)S(1)} %add_rsqrt_fusion, ...), kind=kOutput, calls=%fused_computation.40 | convolution fusion | flops 1679990784 | bytes 9604648 | tf_op jit(solution)/shard_map/while/body/eval_jaxpr/cond/branch_1_fun/dot_general | solution.py:57
  177.1 7.9 %collective-permute-start = (bf16[1,197,1024]{2,1,0:T(8,128)(2,1)S(1)}, bf16[1,197,1024]{2,1,0:T(8,128)(2,1)S(1)}, u32[]{:S(2)}, u32[]{:S(2)}) collective-permute-start(bf16[1,197,1024]{2,1,0:T(8,128)(2,1)S(1)} %get-tuple-element.476), channel_id=1, source_target_pairs={{0,1},{1,2},{2,3},{4,5},{5,6},{6,7},{8,9},{9,10},{10,11},{12,13},{... | collective-permute-start | bytes 1210376 | tf_op jit(solution)/shard_map/while/body/eval_jaxpr/ppermute | solution.py:17
  187.4 22.1 %conditional.2 = (bf16[1,197,1024]{2,1,0:T(8,128)(2,1)S(1)}) conditional(s32[]{:T(128)} %convert_element_type.128, bf16[1,197,1024]{2,1,0:T(8,128)(2,1)S(1)} %bitcast_select_fusion.2, (bf16[1,197,1024]{2,1,0:T(8,128)(2,1)S(1)}, f32[1,1024]{1,0:T(1,128)S(1)}, bf16[1,1024,3072]{2,1,0:T(8,128)(2,1)}, bf16[1,1024,1024]{2,1,0:T(8,128)(2,1)}, ...), branch_computations={%region_1.1_spmd, %region_2.8_spmd} | conditional | flops 3499470848 | bytes 46394252 | solution.py:107
  200.8 8.7 %fusion.40 = bf16[1,197,1024]{2,1,0:T(8,128)(2,1)S(1)} fusion(f32[1,197,1024]{2,1,0:T(8,128)S(1)} %get-tuple-element.344, bf16[1,2048,1024]{2,1,0:T(8,128)(2,1)} %get-tuple-element.295, bf16[1,1024,2048]{2,1,0:T(8,128)(2,1)} %get-tuple-element.294, f32[1024]{0:T(1024)S(1)} %bitcast.93, f32[197]{0:T(256)S(1)} %add_rsqrt_fusion, ...), kind=kOutput, calls=%fused_computation.40 | convolution fusion | flops 1679990784 | bytes 9604648 | tf_op jit(solution)/shard_map/while/body/eval_jaxpr/cond/branch_1_fun/dot_general | solution.py:57
  209.5 7.9 %collective-permute-start = (bf16[1,197,1024]{2,1,0:T(8,128)(2,1)S(1)}, bf16[1,197,1024]{2,1,0:T(8,128)(2,1)S(1)}, u32[]{:S(2)}, u32[]{:S(2)}) collective-permute-start(bf16[1,197,1024]{2,1,0:T(8,128)(2,1)S(1)} %get-tuple-element.476), channel_id=1, source_target_pairs={{0,1},{1,2},{2,3},{4,5},{5,6},{6,7},{8,9},{9,10},{10,11},{12,13},{... | collective-permute-start | bytes 1210376 | tf_op jit(solution)/shard_map/while/body/eval_jaxpr/ppermute | solution.py:17
  219.8 22.1 %conditional.2 = (bf16[1,197,1024]{2,1,0:T(8,128)(2,1)S(1)}) conditional(s32[]{:T(128)} %convert_element_type.128, bf16[1,197,1024]{2,1,0:T(8,128)(2,1)S(1)} %bitcast_select_fusion.2, (bf16[1,197,1024]{2,1,0:T(8,128)(2,1)S(1)}, f32[1,1024]{1,0:T(1,128)S(1)}, bf16[1,1024,3072]{2,1,0:T(8,128)(2,1)}, bf16[1,1024,1024]{2,1,0:T(8,128)(2,1)}, ...), branch_computations={%region_1.1_spmd, %region_2.8_spmd} | conditional | flops 3499470848 | bytes 46394252 | solution.py:107
  233.2 8.7 %fusion.40 = bf16[1,197,1024]{2,1,0:T(8,128)(2,1)S(1)} fusion(f32[1,197,1024]{2,1,0:T(8,128)S(1)} %get-tuple-element.344, bf16[1,2048,1024]{2,1,0:T(8,128)(2,1)} %get-tuple-element.295, bf16[1,1024,2048]{2,1,0:T(8,128)(2,1)} %get-tuple-element.294, f32[1024]{0:T(1024)S(1)} %bitcast.93, f32[197]{0:T(256)S(1)} %add_rsqrt_fusion, ...), kind=kOutput, calls=%fused_computation.40 | convolution fusion | flops 1679990784 | bytes 9604648 | tf_op jit(solution)/shard_map/while/body/eval_jaxpr/cond/branch_1_fun/dot_general | solution.py:57
  242.0 7.9 %collective-permute-start = (bf16[1,197,1024]{2,1,0:T(8,128)(2,1)S(1)}, bf16[1,197,1024]{2,1,0:T(8,128)(2,1)S(1)}, u32[]{:S(2)}, u32[]{:S(2)}) collective-permute-start(bf16[1,197,1024]{2,1,0:T(8,128)(2,1)S(1)} %get-tuple-element.476), channel_id=1, source_target_pairs={{0,1},{1,2},{2,3},{4,5},{5,6},{6,7},{8,9},{9,10},{10,11},{12,13},{... | collective-permute-start | bytes 1210376 | tf_op jit(solution)/shard_map/while/body/eval_jaxpr/ppermute | solution.py:17
  252.3 30.1 %collective-permute-start = (bf16[1,197,1024]{2,1,0:T(8,128)(2,1)S(1)}, bf16[1,197,1024]{2,1,0:T(8,128)(2,1)S(1)}, u32[]{:S(2)}, u32[]{:S(2)}) collective-permute-start(bf16[1,197,1024]{2,1,0:T(8,128)(2,1)S(1)} %get-tuple-element.476), channel_id=1, source_target_pairs={{0,1},{1,2},{2,3},{4,5},{5,6},{6,7},{8,9},{9,10},{10,11},{12,13},{... | collective-permute-start | bytes 1210376 | tf_op jit(solution)/shard_map/while/body/eval_jaxpr/ppermute | solution.py:17
  284.8 7.9 %collective-permute-start = (bf16[1,197,1024]{2,1,0:T(8,128)(2,1)S(1)}, bf16[1,197,1024]{2,1,0:T(8,128)(2,1)S(1)}, u32[]{:S(2)}, u32[]{:S(2)}) collective-permute-start(bf16[1,197,1024]{2,1,0:T(8,128)(2,1)S(1)} %get-tuple-element.476), channel_id=1, source_target_pairs={{0,1},{1,2},{2,3},{4,5},{5,6},{6,7},{8,9},{9,10},{10,11},{12,13},{... | collective-permute-start | bytes 1210376 | tf_op jit(solution)/shard_map/while/body/eval_jaxpr/ppermute | solution.py:17
  295.1 30.1 %collective-permute-start = (bf16[1,197,1024]{2,1,0:T(8,128)(2,1)S(1)}, bf16[1,197,1024]{2,1,0:T(8,128)(2,1)S(1)}, u32[]{:S(2)}, u32[]{:S(2)}) collective-permute-start(bf16[1,197,1024]{2,1,0:T(8,128)(2,1)S(1)} %get-tuple-element.476), channel_id=1, source_target_pairs={{0,1},{1,2},{2,3},{4,5},{5,6},{6,7},{8,9},{9,10},{10,11},{12,13},{... | collective-permute-start | bytes 1210376 | tf_op jit(solution)/shard_map/while/body/eval_jaxpr/ppermute | solution.py:17
  327.3 24.5 %psum.28 = bf16[8,256]{1,0:T(8,128)(2,1)S(1)} all-reduce(bf16[8,256]{1,0:T(8,128)(2,1)S(1)} %fusion.136), channel_id=1, replica_groups=mesh['dp'=8,'section'=4] {'section'}, use_global_device_ids=true, to_apply=%region_13.14 | all-reduce | flops 2048 | bytes 8192 | tf_op jit(solution)/shard_map/psum | solution.py:22
  351.8 32.4 %all_gather.7 = bf16[64,256]{1,0:T(8,128)(2,1)S(1)} all-gather(bf16[8,256]{1,0:T(8,128)(2,1)S(1)} %psum.28), channel_id=1, replica_groups=mesh['dp'=8,'section'=4] {'dp'}, dimensions={0}, use_global_device_ids=true | all-gather | bytes 36864 | tf_op jit(solution)/shard_map/all_gather | solution.py:145
  386.3 30.6 %all_gather.6 = bf16[64,256]{1,0:T(8,128)(2,1)S(1)} all-gather(bf16[8,256]{1,0:T(8,128)(2,1)S(1)} %copy-done.4), channel_id=1, replica_groups=mesh['dp'=8,'section'=4] {'dp'}, dimensions={0}, use_global_device_ids=true | all-gather | bytes 36864 | tf_op jit(solution)/shard_map/all_gather | solution.py:118
  417.3 38.5 %pmax.7 = f32[64]{0:T(128)S(1)} all-reduce(f32[64]{0:T(128)S(1)} %get-tuple-element.347), channel_id=1, replica_groups=mesh['dp'=8,'section'=4] {'dp','section'}, use_global_device_ids=true, to_apply=%region_15.16 | all-reduce | flops 64 | bytes 512 | tf_op jit(solution)/shard_map/pmax | solution.py:125
  456.1 6.6 %psum.29 = f32[64]{0:T(128)S(1)} all-reduce(f32[64]{0:T(128)S(1)} %exponential_reduce_fusion), channel_id=1, replica_groups=mesh['dp'=8,'section'=4] {'section'}, use_global_device_ids=true, to_apply=%region_17.18 | all-reduce | flops 64 | bytes 512 | tf_op jit(solution)/shard_map/psum | solution.py:127
  462.7 19.4 %psum.30 = f32[64]{0:T(128)S(1)} all-reduce(f32[64]{0:T(128)S(1)} %psum.29), channel_id=1, replica_groups=mesh['dp'=8,'section'=4] {'dp'}, use_global_device_ids=true, to_apply=%region_18.19 | all-reduce | flops 64 | bytes 512 | tf_op jit(solution)/shard_map/psum | solution.py:126
  483.3 17.7 %psum.31 = f32[]{:T(128)} all-reduce(f32[]{:T(128)} %get-tuple-element.339), channel_id=1, replica_groups=mesh['dp'=8,'section'=4] {'dp'}, use_global_device_ids=true, to_apply=%region_21.22 | all-reduce | flops 1 | bytes 8 | tf_op jit(solution)/shard_map/psum | solution.py:143
  (195 shorter events, 151.3 us)
Async XLA Ops:
  0.6 326.3 %copy-start = (bf16[1024,256]{1,0:T(8,128)(2,1)S(1)}, bf16[1024,256]{1,0:T(8,128)(2,1)}, u32[]{:S(2)}) copy-start(bf16[1024,256]{1,0:T(8,128)(2,1)} %param.25) | copy-start | bytes 1572868
  0.7 5.5 %copy-start.6 = (f32[1,1024]{1,0:T(1,128)S(1)}, f32[1,1024]{1,0:T(1,128)}, u32[]{:S(2)}) copy-start(f32[1,1024]{1,0:T(1,128)} %param.18) | copy-start | bytes 12292
  0.7 5.5 %copy-start.7 = (f32[1,1024]{1,0:T(1,128)S(1)}, f32[1,1024]{1,0:T(1,128)}, u32[]{:S(2)}) copy-start(f32[1,1024]{1,0:T(1,128)} %param.21) | copy-start | bytes 12292
  6.2 320.7 %copy-start.8 = (f32[1024]{0:T(1024)S(1)}, f32[1024]{0:T(1024)}, u32[]{:S(2)}) copy-start(f32[1024]{0:T(1024)} %param.24) | copy-start | bytes 12292
  6.2 378.7 %copy-start.2 = (bf16[1024,256]{1,0:T(8,128)(2,1)S(1)}, bf16[1024,256]{1,0:T(8,128)(2,1)}, u32[]{:S(2)}) copy-start(bf16[1024,256]{1,0:T(8,128)(2,1)} %param.27) | copy-start | bytes 1572868
  6.2 378.7 %copy-start.5 = (s32[64]{0:T(128)S(1)}, s32[64]{0:T(128)}, u32[]{:S(2)}) copy-start(s32[64]{0:T(128)} %param.28) | copy-start | bytes 772
  18.2 1.6 copy-start.1
  29.5 2.7 collective-permute-start
  44.0 1.6 copy-start.1
  55.3 3.7 collective-permute-start
  70.9 1.6 copy-start.1
  82.2 6.8 %collective-permute-start = (bf16[1,197,1024]{2,1,0:T(8,128)(2,1)S(1)}, bf16[1,197,1024]{2,1,0:T(8,128)(2,1)S(1)}, u32[]{:S(2)}, u32[]{:S(2)}) collective-permute-start(bf16[1,197,1024]{2,1,0:T(8,128)(2,1)S(1)} %get-tuple-element.476), channel_id=1, source_target_pairs={{0,1},{1,2},{2,3},{4,5},{5,6},{6,7},{8,9},{9,10},{10,11},{12,13},{... | collective-permute-start | bytes 1210376 | tf_op jit(solution)/shard_map/while/body/eval_jaxpr/ppermute | solution.py:17
  100.9 1.6 copy-start.1
  112.2 9.3 %collective-permute-start = (bf16[1,197,1024]{2,1,0:T(8,128)(2,1)S(1)}, bf16[1,197,1024]{2,1,0:T(8,128)(2,1)S(1)}, u32[]{:S(2)}, u32[]{:S(2)}) collective-permute-start(bf16[1,197,1024]{2,1,0:T(8,128)(2,1)S(1)} %get-tuple-element.476), channel_id=1, source_target_pairs={{0,1},{1,2},{2,3},{4,5},{5,6},{6,7},{8,9},{9,10},{10,11},{12,13},{... | collective-permute-start | bytes 1210376 | tf_op jit(solution)/shard_map/while/body/eval_jaxpr/ppermute | solution.py:17
  133.3 1.6 copy-start.1
  144.6 9.3 %collective-permute-start = (bf16[1,197,1024]{2,1,0:T(8,128)(2,1)S(1)}, bf16[1,197,1024]{2,1,0:T(8,128)(2,1)S(1)}, u32[]{:S(2)}, u32[]{:S(2)}) collective-permute-start(bf16[1,197,1024]{2,1,0:T(8,128)(2,1)S(1)} %get-tuple-element.476), channel_id=1, source_target_pairs={{0,1},{1,2},{2,3},{4,5},{5,6},{6,7},{8,9},{9,10},{10,11},{12,13},{... | collective-permute-start | bytes 1210376 | tf_op jit(solution)/shard_map/while/body/eval_jaxpr/ppermute | solution.py:17
  165.8 1.6 copy-start.1
  177.1 9.3 %collective-permute-start = (bf16[1,197,1024]{2,1,0:T(8,128)(2,1)S(1)}, bf16[1,197,1024]{2,1,0:T(8,128)(2,1)S(1)}, u32[]{:S(2)}, u32[]{:S(2)}) collective-permute-start(bf16[1,197,1024]{2,1,0:T(8,128)(2,1)S(1)} %get-tuple-element.476), channel_id=1, source_target_pairs={{0,1},{1,2},{2,3},{4,5},{5,6},{6,7},{8,9},{9,10},{10,11},{12,13},{... | collective-permute-start | bytes 1210376 | tf_op jit(solution)/shard_map/while/body/eval_jaxpr/ppermute | solution.py:17
  198.2 1.6 copy-start.1
  209.5 9.3 %collective-permute-start = (bf16[1,197,1024]{2,1,0:T(8,128)(2,1)S(1)}, bf16[1,197,1024]{2,1,0:T(8,128)(2,1)S(1)}, u32[]{:S(2)}, u32[]{:S(2)}) collective-permute-start(bf16[1,197,1024]{2,1,0:T(8,128)(2,1)S(1)} %get-tuple-element.476), channel_id=1, source_target_pairs={{0,1},{1,2},{2,3},{4,5},{5,6},{6,7},{8,9},{9,10},{10,11},{12,13},{... | collective-permute-start | bytes 1210376 | tf_op jit(solution)/shard_map/while/body/eval_jaxpr/ppermute | solution.py:17
  230.7 1.6 copy-start.1
  242.0 9.3 %collective-permute-start = (bf16[1,197,1024]{2,1,0:T(8,128)(2,1)S(1)}, bf16[1,197,1024]{2,1,0:T(8,128)(2,1)S(1)}, u32[]{:S(2)}, u32[]{:S(2)}) collective-permute-start(bf16[1,197,1024]{2,1,0:T(8,128)(2,1)S(1)} %get-tuple-element.476), channel_id=1, source_target_pairs={{0,1},{1,2},{2,3},{4,5},{5,6},{6,7},{8,9},{9,10},{10,11},{12,13},{... | collective-permute-start | bytes 1210376 | tf_op jit(solution)/shard_map/while/body/eval_jaxpr/ppermute | solution.py:17
  252.3 31.4 %collective-permute-start = (bf16[1,197,1024]{2,1,0:T(8,128)(2,1)S(1)}, bf16[1,197,1024]{2,1,0:T(8,128)(2,1)S(1)}, u32[]{:S(2)}, u32[]{:S(2)}) collective-permute-start(bf16[1,197,1024]{2,1,0:T(8,128)(2,1)S(1)} %get-tuple-element.476), channel_id=1, source_target_pairs={{0,1},{1,2},{2,3},{4,5},{5,6},{6,7},{8,9},{9,10},{10,11},{12,13},{... | collective-permute-start | bytes 1210376 | tf_op jit(solution)/shard_map/while/body/eval_jaxpr/ppermute | solution.py:17
  284.8 9.3 %collective-permute-start = (bf16[1,197,1024]{2,1,0:T(8,128)(2,1)S(1)}, bf16[1,197,1024]{2,1,0:T(8,128)(2,1)S(1)}, u32[]{:S(2)}, u32[]{:S(2)}) collective-permute-start(bf16[1,197,1024]{2,1,0:T(8,128)(2,1)S(1)} %get-tuple-element.476), channel_id=1, source_target_pairs={{0,1},{1,2},{2,3},{4,5},{5,6},{6,7},{8,9},{9,10},{10,11},{12,13},{... | collective-permute-start | bytes 1210376 | tf_op jit(solution)/shard_map/while/body/eval_jaxpr/ppermute | solution.py:17
  295.1 31.4 %collective-permute-start = (bf16[1,197,1024]{2,1,0:T(8,128)(2,1)S(1)}, bf16[1,197,1024]{2,1,0:T(8,128)(2,1)S(1)}, u32[]{:S(2)}, u32[]{:S(2)}) collective-permute-start(bf16[1,197,1024]{2,1,0:T(8,128)(2,1)S(1)} %get-tuple-element.476), channel_id=1, source_target_pairs={{0,1},{1,2},{2,3},{4,5},{5,6},{6,7},{8,9},{9,10},{10,11},{12,13},{... | collective-permute-start | bytes 1210376 | tf_op jit(solution)/shard_map/while/body/eval_jaxpr/ppermute | solution.py:17
  326.5 59.7 %copy-start.4 = (bf16[8,256]{1,0:T(8,128)(2,1)S(1)}, bf16[8,256]{1,0:T(8,128)(2,1)}, u32[]{:S(2)}) copy-start(bf16[8,256]{1,0:T(8,128)(2,1)} %param.26) | copy-start | bytes 12292
  351.8 149.9 %copy-start.3 = (bf16[8,256]{1,0:T(8,128)(2,1)}, bf16[8,256]{1,0:T(8,128)(2,1)S(1)}, u32[]{:S(2)}) copy-start(bf16[8,256]{1,0:T(8,128)(2,1)S(1)} %psum.28) | copy-start | bytes 12292
